TPU v7x, 32 devices: a whole 2x2x4 slice. The times are simulated.
32 devices in a mesh: dp: 8 (over y, x, core), tp: 4 (over z).
Axes of the slice: x: 2, y: 2, z: 4, core: 2. Of those that a mesh axis runs over, the one named last changes fastest.
Arguments:
- slope_up: float32 [8, 1280, 5120], P('dp', None, 'tp'), may hold values from -0.875 to 0.875
- slope_down: float32 [8, 5120, 1280], P('dp', 'tp'), may hold values from -0.875 to 0.875
- slope_norm: float32 [8, 1280], P('dp'), may hold values from -8 to 8
- slope_bias: float32 [8, 1280], P('dp'), may hold values from -8 to 8
- param_up: float32 [1280, 5120], P('dp', 'tp'), may hold values from -0.15625 to 0.15625
- param_down: float32 [5120, 1280], P('tp', 'dp'), may hold values from -0.078125 to 0.078125
- param_norm: float32 [1280], P('dp'), may hold values from 0.25 to 1.75
- param_bias: float32 [1280], P('dp'), may hold values from -3 to 3
- state_up: float32 [1280, 5120], P('dp', 'tp'), may hold values from -1.75 to 1.75
- state_down: float32 [5120, 1280], P('tp', 'dp'), may hold values from -1.75 to 1.75
- state_norm: float32 [1280], P('dp'), may hold values from -1.75 to 1.75
- state_bias: float32 [1280], P('dp'), may hold values from -1.75 to 1.75
Outputs:
- half_up: bfloat16 [1280, 5120], P(None, 'tp')
- half_down: bfloat16 [5120, 1280], P('tp')
- half_norm: bfloat16 [1280], replicated
- half_bias: bfloat16 [1280], replicated
- next_up: float32 [1280, 5120], P('dp', 'tp')
- next_down: float32 [5120, 1280], P('tp', 'dp')
- next_norm: float32 [1280], P('dp')
- next_bias: float32 [1280], P('dp')
- state_new_up: float32 [1280, 5120], P('dp', 'tp')
- state_new_down: float32 [5120, 1280], P('tp', 'dp')
- state_new_norm: float32 [1280], P('dp')
- state_new_bias: float32 [1280], P('dp')
All inputs are finite; a program needn't handle non-finite values.
Results may differ from a plain program's by a relative error of at most 0.009.
Values may be sent and summed in bfloat16 or wider, within the bound.
A program may use at most 64 MiB of HBM per device.

v0:
```python
import functools

import jax
import jax.numpy as jnp
from jax import lax
from jax.experimental import pallas as pl
from jax.experimental.pallas import tpu as pltpu
from jax.sharding import PartitionSpec as P

learn_rate = 0.1
hold_rate = 0.7
LANES = 128
F32 = jnp.float32
BF16 = jnp.bfloat16
D2D, RS1, RS2, AG1, AG2, SH1, SH2 = range(7)


def slab_plan(columns):
    half = columns // LANES // 2
    widths = [half - half // 2, half // 2] if half > 1 else [half]
    plan, start = [], 0
    for width in widths:
        for axis in (0, 1):
            plan.append((start, width * LANES, axis))
            start += width * LANES
    return plan


def row_loop(rows, step, fn):
    def go(i, carry):
        fn(pl.ds(pl.multiple_of(i * step, step), step))
        return carry

    lax.fori_loop(0, rows // step, go, 0)


def kernel(
    replicas, plan,
    su, sd, sn, sb, pu, pd, pn, pb, tu, td, tn, tb,
    hu_out, hd_out, nu_out, nd_out, tu_out, td_out, vec_out, vech_out,
    fu, fd, bu, bd, r0, r1, r2, gu, gd, par, sta, vsend, vrecv, hd,
    send_sem, recv_sem, vsend_sem, vrecv_sem, load_sem, par_sem, out_sem, st_sem,
):
    chunk, columns = pu.shape
    width = replicas * chunk
    me = lax.axis_index("dp")
    c = lax.rem(me, 2)
    x = lax.rem(me // 2, 2)
    y = me // 4
    mate = me + 1 - 2 * c
    nbr = (me + 2 - 4 * x, me + 4 - 8 * y)
    rate = replicas ** (-0.5)
    slabs = [(m,) + s for m in (0, 1) for s in plan]
    per = len(plan)
    step = 32 if chunk % 32 == 0 else 16
    b, g = (bu, bd), (gu, gd)

    loads = []
    for i, (m, lo, w, _) in enumerate(slabs):
        if m == 0:
            cp = pltpu.make_async_copy(su.at[0, :, pl.ds(lo, w)], fu.at[:, pl.ds(lo, w)], load_sem.at[i])
        else:
            cp = pltpu.make_async_copy(sd.at[0, pl.ds(lo, w)], fd.at[pl.ds(lo, w)], load_sem.at[i])
        cp.start()
        loads.append(cp)
    ploads = []
    for i, (src, dst) in enumerate(((pu, par.at[0]), (pd, par.at[1]), (tu, sta.at[0]), (td, sta.at[1]))):
        cp = pltpu.make_async_copy(src, dst, par_sem.at[i])
        cp.start()
        ploads.append(cp)

    barrier = pltpu.get_barrier_semaphore()
    for i in range(1, replicas):
        pl.semaphore_signal(
            barrier, inc=1, device_id={"dp": lax.rem(me + i, replicas)}, device_id_type=pl.DeviceIdType.MESH
        )

    vw = columns_pad(chunk)
    vsend[...] = jnp.zeros_like(vsend)
    for row, (slope, param, state) in enumerate(((sn, pn, tn), (sb, pb, tb))):
        vsend[row : row + 1, 0:width] = slope[...]
        vsend[row : row + 1, width : width + chunk] = param[...]
        vsend[row : row + 1, width + vw : width + vw + chunk] = state[...]
    vrecv[me] = vsend[...]

    def convert(i):
        m, lo, w, _ = slabs[i]
        loads[i].wait()
        if m == 0:
            for k in range(replicas):
                dst = bu.at[k // 4, (k // 2) % 2, k % 2]

                def go(rows, k=k, dst=dst):
                    src = pl.ds(pl.multiple_of(k * chunk + rows.start, step), step)
                    dst[rows, lo : lo + w] = fu[src, lo : lo + w].astype(BF16)

                row_loop(chunk, step, go)
        else:
            for block in range(width // LANES):
                first = block * LANES
                turned = fd[lo : lo + w, first : first + LANES].T.astype(BF16)
                done = 0
                while done < LANES:
                    k, off = divmod(first + done, chunk)
                    n = min(LANES - done, chunk - off)
                    bd[k // 4, (k // 2) % 2, k % 2, off : off + n, lo : lo + w] = turned[done : done + n]
                    done += n

    def copy(i, kind, src, dst, target):
        cp = pltpu.make_async_remote_copy(
            src_ref=src, dst_ref=dst,
            send_sem=send_sem.at[kind, i], recv_sem=recv_sem.at[kind, i],
            device_id={"dp": target}, device_id_type=pl.DeviceIdType.MESH,
        )
        cp.start()
        return cp

    copies = {}

    def swap(i):
        m, lo, w, _ = slabs[i]
        cols = pl.ds(lo, w)
        copies[i, D2D] = copy(i, D2D, b[m].at[:, :, 1 - c, :, cols], r0.at[m, :, :, :, cols], mate)

    def add_to(dst, src, lo, w):
        def go(rows):
            cols = slice(lo, lo + w)
            dst[rows, cols] = (dst[rows, cols].astype(F32) + src[rows, cols].astype(F32)).astype(BF16)

        row_loop(chunk, step, go)

    def rs1(i):
        m, lo, w, axis = slabs[i]
        cols = pl.ds(lo, w)
        copies[i, D2D].wait_recv()
        for far in (1, 0):
            for j in (0, 1):
                if axis == 0:
                    yy, xx = j, (1 - x if far else x)
                else:
                    yy, xx = (1 - y if far else y), j
                add_to(b[m].at[yy, xx, c], r0.at[m, yy, xx], lo, w)
            if far:
                src = b[m].at[:, 1 - x, c, :, cols] if axis == 0 else b[m].at[1 - y, :, c, :, cols]
                copies[i, RS1] = copy(i, RS1, src, r1.at[m, :, :, cols], nbr[axis])

    def rs2(i):
        m, lo, w, axis = slabs[i]
        cols = pl.ds(lo, w)
        copies[i, RS1].wait_recv()
        j = 1 - y if axis == 0 else 1 - x
        far = b[m].at[1 - y, x, c] if axis == 0 else b[m].at[y, 1 - x, c]
        add_to(far, r1.at[m, j], lo, w)
        copies[i, RS2] = copy(i, RS2, far.at[:, cols], r2.at[m, :, cols], nbr[1 - axis])
        add_to(b[m].at[y, x, c], r1.at[m, 1 - j], lo, w)

    stores = []

    def update(i):
        m, lo, w, axis = slabs[i]
        cs = slice(lo, lo + w)
        cols = pl.ds(lo, w)
        copies[i, RS2].wait_recv()
        own, out = b[m].at[y, x, c], g[m].at[y, x, c]

        def go(rows):
            mean = (own[rows, cs].astype(F32) + r2[m, rows, cs].astype(F32)) * rate
            state = hold_rate * sta[m, rows, cs] + mean
            new = par[m, rows, cs] - learn_rate * state
            out[rows, cs] = new.astype(BF16)
            sta[m, rows, cs] = state
            par[m, rows, cs] = new

        row_loop(chunk, step, go)
        copies[i, AG1] = copy(i, AG1, out.at[:, cols], out.at[:, cols], nbr[1 - axis])
        for n, (src, dst) in enumerate(((par, (nu_out, nd_out)[m]), (sta, (tu_out, td_out)[m]))):
            cp = pltpu.make_async_copy(src.at[m, :, cols], dst.at[:, cols], st_sem.at[n, i])
            cp.start()
            stores.append(cp)

    def ag2(i):
        m, lo, w, axis = slabs[i]
        cols = pl.ds(lo, w)
        copies[i, AG1].wait_recv()
        part = g[m].at[:, x, c, :, cols] if axis == 0 else g[m].at[y, :, c, :, cols]
        copies[i, AG2] = copy(i, AG2, part, part, nbr[axis])
        copies[i, SH1] = copy(i, SH1, part, part, mate)

    def share(i):
        m, lo, w, axis = slabs[i]
        cols = pl.ds(lo, w)
        copies[i, AG2].wait_recv()
        part = g[m].at[:, 1 - x, c, :, cols] if axis == 0 else g[m].at[1 - y, :, c, :, cols]
        copies[i, SH2] = copy(i, SH2, part, part, mate)

    def finish(i):
        m, lo, w, axis = slabs[i]
        cols = pl.ds(lo, w)
        copies[i, SH1].wait_recv()
        copies[i, SH2].wait_recv()
        if m == 0:
            cp = pltpu.make_async_copy(gu.at[:, :, :, :, cols], hu_out.at[:, :, :, :, cols], out_sem.at[i])
        else:
            for block in range(width // LANES):
                first, done, parts = block * LANES, 0, []
                while done < LANES:
                    k, off = divmod(first + done, chunk)
                    n = min(LANES - done, chunk - off)
                    parts.append(gd[k // 4, (k // 2) % 2, k % 2, off : off + n, lo : lo + w].astype(F32))
                    done += n
                whole = parts[0] if len(parts) == 1 else jnp.concatenate(parts, axis=0)
                hd[lo : lo + w, first : first + LANES] = whole.T.astype(BF16)
            cp = pltpu.make_async_copy(hd.at[cols], hd_out.at[cols], out_sem.at[i])
        cp.start()
        stores.append(cp)

    count = len(slabs)
    convert(0)
    pl.semaphore_wait(barrier, replicas - 1)
    swap(0)
    vcopies = []
    for i in range(1, replicas):
        to = lax.rem(me + i, replicas)
        cp = pltpu.make_async_remote_copy(
            src_ref=vsend, dst_ref=vrecv.at[me],
            send_sem=vsend_sem.at[i], recv_sem=vrecv_sem.at[i],
            device_id={"dp": to}, device_id_type=pl.DeviceIdType.MESH,
        )
        cp.start()
        vcopies.append(cp)
    convert(1)
    swap(1)
    for i in range(2, count):
        rs1(i - 2)
        convert(i)
        swap(i)
    rs1(count - 2)
    rs1(count - 1)

    for cp in vcopies:
        cp.wait_recv()
    total = vrecv[0, :, 0:width]
    for k in range(1, replicas):
        total = total + vrecv[k, :, 0:width]
    lane = lax.broadcasted_iota(jnp.int32, (2, width), 1)

    def whole(at):
        full = jnp.zeros((2, width), F32)
        for k in range(replicas):
            piece = vrecv[k, :, at : at + vw]
            wide = jnp.concatenate([piece, jnp.zeros((2, width - vw), F32)], axis=1) if width > vw else piece
            moved = pltpu.roll(wide, k * chunk, 1) if k else wide
            full = jnp.where((lane >= k * chunk) & (lane < (k + 1) * chunk), moved, full)
        return full

    vstate = hold_rate * whole(width + vw) + total * rate
    vnext = whole(width) - learn_rate * vstate
    vech_out[...] = vnext.astype(BF16)
    vec_out[0] = vnext
    vec_out[1] = vstate

    for i in range(count):
        rs2(i)
    for cp in ploads:
        cp.wait()
    for i in range(count):
        update(i)
    order = list(range(per // 2)) + list(range(per, count)) + list(range(per // 2, per))
    for i in order:
        ag2(i)
    for n, i in enumerate(order):
        share(i)
        if n:
            finish(order[n - 1])
    finish(order[-1])
    for cp in copies.values():
        cp.wait_send()
    for cp in vcopies:
        cp.wait_send()
    for cp in stores:
        cp.wait()


def columns_pad(n):
    return -(-n // LANES) * LANES


def fused(slope_up, slope_down, slope_norm, slope_bias, param_up, param_down, param_norm, param_bias,
          state_up, state_down, state_norm, state_bias):
    replicas = lax.axis_size("dp")
    chunk, columns = param_up.shape
    width = replicas * chunk
    plan = slab_plan(columns)
    count = 2 * len(plan)
    vw = columns_pad(chunk)
    hbm = pl.BlockSpec(memory_space=pl.ANY)
    vmem = pl.BlockSpec(memory_space=pltpu.VMEM)
    cube = (2, 2, 2, chunk, columns)
    shape = jax.ShapeDtypeStruct
    dma = pltpu.SemaphoreType.DMA
    row = lambda v: v.reshape(1, -1)
    hu, hd, nu, nd, tu, td, vec, vech = pl.pallas_call(
        functools.partial(kernel, replicas, plan),
        out_shape=(
            shape(cube, BF16), shape((columns, width), BF16),
            shape((chunk, columns), F32), shape((chunk, columns), F32),
            shape((chunk, columns), F32), shape((chunk, columns), F32),
            shape((2, 2, width), F32), shape((2, width), BF16),
        ),
        in_specs=[hbm, hbm, vmem, vmem, hbm, hbm, vmem, vmem, hbm, hbm, vmem, vmem],
        out_specs=[hbm] * 6 + [vmem] * 2,
        scratch_shapes=[
            pltpu.VMEM((width, columns), F32), pltpu.VMEM((columns, width), F32),
            pltpu.VMEM(cube, BF16), pltpu.VMEM(cube, BF16),
            pltpu.VMEM((2, 2, 2, chunk, columns), BF16),
            pltpu.VMEM((2, 2, chunk, columns), BF16),
            pltpu.VMEM((2, chunk, columns), BF16),
            pltpu.VMEM(cube, BF16), pltpu.VMEM(cube, BF16),
            pltpu.VMEM((2, chunk, columns), F32), pltpu.VMEM((2, chunk, columns), F32),
            pltpu.VMEM((2, width + 2 * vw), F32), pltpu.VMEM((replicas, 2, width + 2 * vw), F32),
            pltpu.VMEM((columns, width), BF16),
            dma((7, count)), dma((7, count)), dma((replicas,)), dma((replicas,)),
            dma((count,)), dma((4,)), dma((count,)), dma((2, count)),
        ],
        compiler_params=pltpu.CompilerParams(collective_id=0, has_side_effects=True),
    )(
        slope_up, slope_down, slope_norm, slope_bias,
        param_up, param_down.T, row(param_norm), row(param_bias),
        state_up, state_down.T, row(state_norm), row(state_bias),
    )
    place = lax.axis_index("dp") * chunk
    own = lax.dynamic_slice_in_dim(vec, place, chunk, axis=2)
    return (
        hu.reshape(width, columns), hd, vech[0], vech[1],
        nu, nd.T, own[0, 0], own[0, 1],
        tu, td.T, own[1, 0], own[1, 1],
    )


def plain(slope_up, slope_down, slope_norm, slope_bias, param_up, param_down, param_norm, param_bias,
          state_up, state_down, state_norm, state_bias):
    rate = lax.axis_size("dp") ** (-0.5)
    place = lax.axis_index("dp")

    def step(mean, param, state):
        state_new = hold_rate * state + mean * rate
        return param - learn_rate * state_new, state_new

    def scattered(slope, dim):
        return lax.psum_scatter(slope[0].astype(BF16), "dp", scatter_dimension=dim, tiled=True).astype(F32)

    def gathered(value, dim):
        return lax.all_gather(value.astype(BF16), "dp", axis=dim, tiled=True)

    sums = lax.psum((slope_norm[0], slope_bias[0]), "dp")
    size = param_norm.shape[0]
    own = [lax.dynamic_slice_in_dim(v, place * size, size) for v in sums]
    nu, tu = step(scattered(slope_up, 0), param_up, state_up)
    nd, td = step(scattered(slope_down, 1), param_down, state_down)
    nn, tn = step(own[0], param_norm, state_norm)
    nb, tb = step(own[1], param_bias, state_bias)
    halves = gathered(nu, 0), gathered(nd, 1), gathered(nn, 0), gathered(nb, 0)
    return halves + (nu, nd, nn, nb, tu, td, tn, tb)


def body(*args):
    replicas = lax.axis_size("dp")
    chunk, columns = args[4].shape
    fits = replicas == 2 ** 3 and chunk % 16 == 0 and columns % (2 * LANES) == 0
    fits = fits and (replicas * chunk) % LANES == 0
    return (fused if fits else plain)(*args)


def solution(mesh):
    matrices = (P("dp", "tp"), P("tp", "dp"), P("dp"), P("dp"))
    return jax.shard_map(
        body,
        mesh=mesh,
        in_specs=(P("dp", None, "tp"), P("dp", "tp", None), P("dp", None), P("dp", None)) + matrices * 2,
        out_specs=(P(None, "tp"), P("tp", None), P(), P()) + matrices * 2,
        check_vma=False,
    )
```

profile of v0, /device:TPU:0, one launch (start us, length us, event | category | flops | bytes accessed | tf_op | source)
XLA Modules:
  0.0 78.6 jit_solution(738926902558177551)
XLA Ops:
  0.6 65.8 %shard_map.211 = (bf16[2,2,2,160,1280]{4,3,2,1,0:T(8,128)(2,1)}, bf16[1280,1280]{1,0:T(8,128)(2,1)}, f32[160,1280]{1,0:T(8,128)}, f32[160,1280]{1,0:T(8,128)}, f...) custom-call(f32[1,1280,1280]{2,1,0:T(8,128)} %su.1, ...), custom_call_target="tpu_custom_call" | custom-call | tf_op jit(solution)/shard_map/pallas_call | solution.py:302
  66.5 1.4 %fusion = (f32[1,1,160]{2,1,0:T(1,128)}, f32[1,1,160]{2,1,0:T(1,128)}, f32[1,1,160]{2,1,0:T(1,128)}, f32[1,1,160]{2,1,0:T(1,128)}) fusion(f32[2,2,1280]{2,1,0:T(2,128)} %get-tuple-element.25, s32[]{:T(128)S(6)} %add.6, s32[]{:T(128)S(6)} %select_n.3), kind=kLoop, calls=%fused_computation.5 | loop fusion | bytes 5128 | tf_op jit(solution)/shard_map/slice | solution.py:336
  67.9 1.4 %slice_reduce_fusion = (bf16[1280]{0:T(1024)(128)(2,1)}, bf16[1280]{0:T(1024)(128)(2,1)}) fusion(bf16[2,1280]{1,0:T(2,128)(2,1)} %get-tuple-element.22), kind=kLoop, calls=%fused_computation | loop fusion | bytes 10240 | tf_op jit(solution)/shard_map/slice | solution.py:334
  69.3 0.0 copy-start
  69.3 4.0 %copy.30 = bf16[1280,1280]{1,0:T(8,128)(2,1)} copy(bf16[1280,1280]{1,0:T(8,128)(2,1)} %bitcast.13) | data formatting | bytes 6553600
  73.3 0.0 copy-done
  73.3 0.0 copy-start.4
  73.3 0.0 copy-start.3
  73.3 1.7 %copy.31 = bf16[1280,1280]{1,0:T(8,128)(2,1)} copy(bf16[1280,1280]{1,0:T(8,128)(2,1)S(1)} %copy-done) | data formatting | bytes 6553600
  75.0 0.0 copy-done.4
  75.0 0.0 copy-start.2
  75.0 0.0 copy-start.1
  75.0 0.9 %copy.32 = f32[160,1280]{1,0:T(8,128)} copy(f32[160,1280]{1,0:T(8,128)S(1)} %copy-done.4) | data formatting | bytes 1638400
  75.9 0.0 copy-done.3
  75.9 0.9 %copy.33 = f32[1280,160]{0,1:T(8,128)} copy(f32[1280,160]{0,1:T(8,128)S(1)} %bitcast.15) | data formatting | bytes 1638400
  76.8 0.0 copy-done.2
  76.8 0.9 %copy.34 = f32[160,1280]{1,0:T(8,128)} copy(f32[160,1280]{1,0:T(8,128)S(1)} %copy-done.2) | data formatting | bytes 1638400
  77.7 0.0 copy-done.1
  77.7 0.9 %copy.35 = f32[1280,160]{0,1:T(8,128)} copy(f32[1280,160]{0,1:T(8,128)S(1)} %bitcast.14) | data formatting | bytes 1638400
Async XLA Ops:
  69.3 4.0 %copy-start = (bf16[1280,1280]{1,0:T(8,128)(2,1)S(1)}, bf16[1280,1280]{1,0:T(8,128)(2,1)}, u32[]{:S(2)}) copy-start(bf16[1280,1280]{1,0:T(8,128)(2,1)} %get-tuple-element.47) | copy-start | bytes 9830404
  73.3 1.7 %copy-start.4 = (f32[160,1280]{1,0:T(8,128)S(1)}, f32[160,1280]{1,0:T(8,128)}, u32[]{:S(2)}) copy-start(f32[160,1280]{1,0:T(8,128)} %get-tuple-element.50) | copy-start | bytes 2457604
  73.3 2.6 %copy-start.3 = (f32[160,1280]{1,0:T(8,128)S(1)}, f32[160,1280]{1,0:T(8,128)}, u32[]{:S(2)}) copy-start(f32[160,1280]{1,0:T(8,128)} %get-tuple-element.24) | copy-start | bytes 2457604
  75.0 1.8 %copy-start.2 = (f32[160,1280]{1,0:T(8,128)S(1)}, f32[160,1280]{1,0:T(8,128)}, u32[]{:S(2)}) copy-start(f32[160,1280]{1,0:T(8,128)} %get-tuple-element.54) | copy-start | bytes 2457604
  75.0 2.7 %copy-start.1 = (f32[160,1280]{1,0:T(8,128)S(1)}, f32[160,1280]{1,0:T(8,128)}, u32[]{:S(2)}) copy-start(f32[160,1280]{1,0:T(8,128)} %get-tuple-element.27) | copy-start | bytes 2457604
where the time goes:
time: 78.9 us; the launch traced here: 78.6 us
  Pallas kernels  65.8 us (83%)
  local copies, waits for them, and re-layouts  12.1 us (15%)
    pallas_call x1, Pallas kernels, fused(): pl.pallas_call(functools.partial(kernel, replicas, plan), out_shape=(shap...  65.8 us
    unnamed x16, local copies, waits for them, and re-layouts  9.28 us

commit v1 on v0

v1 whole, which is shorter than its diff:
```python
import functools
import math

import jax
import jax.numpy as jnp
from jax import lax
from jax.experimental import pallas as pl
from jax.experimental.pallas import tpu as pltpu
from jax.sharding import PartitionSpec as P

learn_rate = 0.1
hold_rate = 0.7
LANES = 128
GRANT_EXTRA = 2 * 1024 * 1024
F32 = jnp.float32
BF16 = jnp.bfloat16
D2D, RS1, RS2, AG1, AG2, SH1, SH2 = range(7)


def widths_of(half, small):
    if half < 2:
        return [half]
    if small:
        return [1] + widths_of(half - 1, False)
    return [half - half // 2, half // 2]


def slab_plan(columns):
    half = columns // LANES // 2
    slabs = []
    for m in (0, 1):
        start = 0
        for width in widths_of(half, m == 0):
            for axis in (0, 1):
                slabs.append((m, start, width * LANES, axis))
                start += width * LANES
    return slabs


def spot(k):
    y, x, core = k // 4, (k // 2) % 2, k % 2
    return (x, y, core) if core else (y, x, core)


def row_loop(rows, step, fn):
    def go(i, carry):
        fn(pl.ds(pl.multiple_of(i * step, step), step))
        return carry

    lax.fori_loop(0, rows // step, go, 0)


def kernel(
    replicas, slabs, order,
    su, sd, sn, sb, pu, pd, pn, pb, tu, td, tn, tb,
    gu, hd, par, sta, vg, vown,
    fu, fd, bu, bd, r0, r1, r2, gd, vin, vpar, vsta, vb, vr0, vr1, vr2,
    send_sem, recv_sem, vsend_sem, vrecv_sem, load_sem, par_sem, vec_sem,
):
    chunk, columns = pu.shape
    width = replicas * chunk
    me = lax.axis_index("dp")
    c = lax.rem(me, 2)
    x = lax.rem(me // 2, 2)
    y = me // 4
    mate = me + 1 - 2 * c
    x_peer, y_peer = me + 2 - 4 * x, me + 4 - 8 * y
    slow, fast = y + c * (x - y), x + c * (y - x)
    nbr = (x_peer + c * (y_peer - x_peer), y_peer + c * (x_peer - y_peer))
    rate = replicas ** (-0.5)
    step = 32 if chunk % 32 == 0 else 16
    count = len(slabs)
    b, g = (bu, bd), (gu, gd)
    V = count

    barrier = pltpu.get_barrier_semaphore()
    for peer in (mate,) + nbr:
        pl.semaphore_signal(barrier, inc=1, device_id={"dp": peer}, device_id_type=pl.DeviceIdType.MESH)

    def local(src, dst, sem):
        cp = pltpu.make_async_copy(src, dst, sem)
        cp.start()
        return cp

    loads = []
    for i, (m, lo, w, _) in enumerate(slabs):
        if m == 0:
            loads.append(local(su.at[0, :, pl.ds(lo, w)], fu.at[:, pl.ds(lo, w)], load_sem.at[i]))
        else:
            loads.append(local(sd.at[0, pl.ds(lo, w)], fd.at[pl.ds(lo, w)], load_sem.at[i]))
    for n, (whole, pair) in enumerate(((vin, (sn, sb)), (vpar, (pn, pb)), (vsta, (tn, tb)))):
        for row in (0, 1):
            local(pair[row], whole.at[row], vec_sem.at[n])
    for n, (whole, pair) in enumerate(((par, (pu, pd)), (sta, (tu, td)))):
        for m in (0, 1):
            local(pair[m], whole.at[m], par_sem.at[n])

    def loaded(sem, *wholes):
        for n, whole in enumerate(wholes):
            pltpu.make_async_copy(whole, whole, sem.at[n]).wait()

    def convert(i):
        m, lo, w, _ = slabs[i]
        loads[i].wait()
        if m == 0:
            for k in range(replicas):
                bu[*spot(k), :, lo : lo + w] = fu[k * chunk : (k + 1) * chunk, lo : lo + w].astype(BF16)
        else:
            for block in range(width // LANES):
                first = block * LANES
                turned = fd[lo : lo + w, first : first + LANES].T.astype(BF16)
                done = 0
                while done < LANES:
                    k, off = divmod(first + done, chunk)
                    n = min(LANES - done, chunk - off)
                    bd[*spot(k), off : off + n, lo : lo + w] = turned[done : done + n]
                    done += n

    share_of = {D2D: 0, AG1: 0, RS1: 1, AG2: 1, RS2: 2, SH1: 3, SH2: 3}
    vec_out = {D2D: 0, AG2: 0, SH1: 0, RS1: 1, SH2: 1, RS2: 2, AG1: 2}
    vec_in = {D2D: 0, AG1: 0, RS1: 1, AG2: 4, RS2: 2, SH1: 3, SH2: 3}

    def remote(i, kind, src, dst, target):
        if i == V:
            sems = vsend_sem.at[vec_out[kind]], vrecv_sem.at[vec_in[kind]]
        else:
            sems = send_sem.at[kind], recv_sem.at[share_of[kind], i ^ 1 if kind == AG2 else i]
        return pltpu.make_async_remote_copy(
            src_ref=src, dst_ref=dst, send_sem=sems[0], recv_sem=sems[1],
            device_id={"dp": target}, device_id_type=pl.DeviceIdType.MESH,
        )

    copies = {}

    def copy(i, kind, src, dst, target):
        copies[i, kind] = remote(i, kind, src, dst, target)
        copies[i, kind].start()

    def sent(kind, whole):
        remote(0, kind, whole, whole, mate).wait_send()

    def swap(i):
        m, lo, w, _ = slabs[i]
        cols = pl.ds(lo, w)
        copy(i, D2D, b[m].at[:, :, 1 - c, :, cols], r0.at[m, :, :, :, cols], mate)

    def add_to(dst, src, lo, w):
        cols = slice(lo, lo + w)
        dst[:, cols] = dst[:, cols] + src[:, cols]

    def rs1(i, swap_next=None):
        m, lo, w, axis = slabs[i]
        cols = pl.ds(lo, w)
        copies[i, D2D].wait_recv()
        for far in (1, 0):
            for j in (0, 1):
                at = (j, 1 - fast if far else fast) if axis == 0 else (1 - slow if far else slow, j)
                add_to(b[m].at[*at, c], r0.at[m, *at], lo, w)
            if far:
                src = b[m].at[:, 1 - fast, c, :, cols] if axis == 0 else b[m].at[1 - slow, :, c, :, cols]
                copy(i, RS1, src, r1.at[m, :, :, cols], nbr[axis])
                if swap_next is not None:
                    swap(swap_next)

    def rs2(i):
        m, lo, w, axis = slabs[i]
        cols = pl.ds(lo, w)
        copies[i, RS1].wait_recv()
        j = 1 - slow if axis == 0 else 1 - fast
        far = b[m].at[1 - slow, fast, c] if axis == 0 else b[m].at[slow, 1 - fast, c]
        add_to(far, r1.at[m, j], lo, w)
        copy(i, RS2, far.at[:, cols], r2.at[m, :, cols], nbr[1 - axis])
        add_to(b[m].at[slow, fast, c], r1.at[m, 1 - j], lo, w)

    def update(i):
        m, lo, w, axis = slabs[i]
        cs = slice(lo, lo + w)
        cols = pl.ds(lo, w)
        copies[i, RS2].wait_recv()
        own, out = b[m].at[slow, fast, c], g[m].at[slow, fast, c]

        def go(rows):
            mean = (own[rows, cs].astype(F32) + r2[m, rows, cs].astype(F32)) * rate
            state = hold_rate * sta[m, rows, cs] + mean
            new = par[m, rows, cs] - learn_rate * state
            out[rows, cs] = new.astype(BF16)
            sta[m, rows, cs] = state
            par[m, rows, cs] = new

        row_loop(chunk, step, go)
        copy(i, AG1, out.at[:, cols], out.at[:, cols], nbr[1 - axis])

    def ag2(i):
        m, lo, w, axis = slabs[i]
        cols = pl.ds(lo, w)
        copies[i, AG1].wait_recv()
        part = g[m].at[:, fast, c, :, cols] if axis == 0 else g[m].at[slow, :, c, :, cols]
        copy(i, AG2, part, part, nbr[axis])
        copy(i, SH1, part, part, mate)

    def share(i):
        m, lo, w, axis = slabs[i]
        cols = pl.ds(lo, w)
        copies[i, AG2].wait_recv()
        part = g[m].at[:, 1 - fast, c, :, cols] if axis == 0 else g[m].at[1 - slow, :, c, :, cols]
        copy(i, SH2, part, part, mate)

    def finish(i):
        m, lo, w, axis = slabs[i]
        both = g[m].at[:, :, 1 - c, :, pl.ds(lo, w)]
        remote(i, SH2, both, both, mate).wait_recv()
        if m == 1:
            for block in range(width // LANES):
                first, done, parts = block * LANES, 0, []
                while done < LANES:
                    k, off = divmod(first + done, chunk)
                    n = min(LANES - done, chunk - off)
                    parts.append(gd[*spot(k), off : off + n, lo : lo + w].astype(F32))
                    done += n
                whole = parts[0] if len(parts) == 1 else jnp.concatenate(parts, axis=0)
                hd[lo : lo + w, first : first + LANES] = whole.T.astype(BF16)

    def vec_swap():
        loaded(vec_sem, vin, vpar, vsta)
        for row in (0, 1):
            for k in range(replicas):
                vb[*spot(k), row : row + 1, 0:chunk] = vin[row, :, k * chunk : (k + 1) * chunk]
        copy(V, D2D, vb.at[:, :, 1 - c], vr0, mate)

    def vec_rs1():
        copies[V, D2D].wait_recv()
        for at in ((0, 0), (0, 1), (1, 0), (1, 1)):
            vb[*at, c] = vb[*at, c] + vr0[*at]
        copy(V, RS1, vb.at[:, 1 - fast, c], vr1, nbr[0])

    def vec_rs2():
        copies[V, RS1].wait_recv()
        for j in (0, 1):
            vb[j, fast, c] = vb[j, fast, c] + vr1[j]
        copy(V, RS2, vb.at[1 - slow, fast, c], vr2, nbr[1])

    def vec_update():
        copies[V, RS2].wait_recv()
        mean = (vb[slow, fast, c] + vr2[...]) * rate
        for row in (0, 1):
            state = hold_rate * vsta[row] + mean[row : row + 1, 0:chunk]
            new = vpar[row] - learn_rate * state
            vg[slow, fast, c, row : row + 1, 0:chunk] = new
            vown[row] = new
            vown[2 + row] = state
        copy(V, AG1, vg.at[slow, fast, c], vg.at[slow, fast, c], nbr[1])

    def vec_ag2():
        copies[V, AG1].wait_recv()
        part = vg.at[:, fast, c]
        copy(V, AG2, part, part, nbr[0])
        copy(V, SH1, part, part, mate)

    def vec_share():
        copies[V, AG2].wait_recv()
        part = vg.at[:, 1 - fast, c]
        copy(V, SH2, part, part, mate)

    vb[...] = jnp.zeros_like(vb)
    vg[slow, fast, c] = jnp.zeros(vr2.shape, F32)
    convert(0)
    pl.semaphore_wait(barrier, 3)
    swap(0)
    convert(1)
    swap(1)
    for i in range(2, count):
        convert(i)
        rs1(i - 2, i)
        if i == 6:
            vec_swap()
        if i == 8:
            vec_rs1()
    rs1(count - 2)
    rs1(count - 1)

    for i in range(count):
        rs2(i)
        if i == 4:
            sent(D2D, r0)
            vec_rs2()
    loaded(par_sem, par, sta)
    for n, i in enumerate(list(range(2, count)) + [0, 1]):
        update(i)
        if n == 0:
            vec_update()
            sent(RS1, r1)
    for n, i in enumerate(order):
        ag2(i)
        if n == 0:
            vec_ag2()
            sent(RS2, r2)
    for n, i in enumerate(order):
        share(i)
        if n == 0:
            sent(AG1, r2)
        if n == 1:
            vec_share()
        if n:
            finish(order[n - 1])
    other = vg.at[:, :, 1 - c]
    remote(V, SH2, other, other, mate).wait_recv()
    for whole, kind in ((vb, D2D), (vr0, RS1), (vr1, RS2)):
        remote(V, kind, whole, whole, mate).wait_send()
    sent(SH1, r1)
    sent(AG2, r1)
    finish(order[-1])
    sent(SH2, r1)


def spill(
    replicas, chunk,
    hu, hd, par, sta, vg, vown,
    hu_out, hd_out, nu_out, nd_out, tu_out, td_out, nn_out, nb_out, tn_out, tb_out, hn_out, hb_out,
    hv0, hv1, sem,
):
    width = replicas * chunk
    vw = columns_pad(chunk)
    for k in range(replicas):
        pltpu.make_async_copy(hu.at[*spot(k)], hu_out.at[pl.ds(k * chunk, chunk)], sem.at[0]).start()
    moves = [
        (hd, hd_out), (par.at[0], nu_out), (par.at[1], nd_out), (sta.at[0], tu_out), (sta.at[1], td_out),
        (vown.at[0], nn_out), (vown.at[1], nb_out), (vown.at[2], tn_out), (vown.at[3], tb_out),
        (hv0, hn_out), (hv1, hb_out),
    ]
    stores = [pltpu.make_async_copy(src, dst, sem.at[i + 1]) for i, (src, dst) in enumerate(moves)]
    for cp in stores[:-2]:
        cp.start()
    lane = lax.broadcasted_iota(jnp.int32, (2, width), 1)
    full = jnp.zeros((2, width), F32)
    for k in range(replicas):
        piece = vg[*spot(k)]
        wide = jnp.concatenate([piece, jnp.zeros((2, width - vw), F32)], axis=1) if width > vw else piece
        moved = pltpu.roll(wide, k * chunk, 1) if k else wide
        full = jnp.where((lane >= k * chunk) & (lane < (k + 1) * chunk), moved, full)
    for row, out in enumerate((hv0, hv1)):
        out[...] = full[row].astype(BF16)
    for cp in stores[-2:]:
        cp.start()
    for cp in stores:
        cp.wait()
    pltpu.make_async_copy(hu_out, hu_out, sem.at[0]).wait()


def columns_pad(n):
    return -(-n // LANES) * LANES


def fused(slope_up, slope_down, slope_norm, slope_bias, param_up, param_down, param_norm, param_bias,
          state_up, state_down, state_norm, state_bias):
    replicas = lax.axis_size("dp")
    chunk, columns = param_up.shape
    width = replicas * chunk
    slabs = slab_plan(columns)
    count = len(slabs)
    per = len([s for s in slabs if s[0] == 0])
    order = list(range(2, 4)) + list(range(per, count)) + list(range(4, per)) + [0, 1]
    vw = columns_pad(chunk)
    hbm = pl.BlockSpec(memory_space=pl.ANY)
    vmem = pl.BlockSpec(memory_space=pltpu.VMEM)
    cube = (2, 2, 2, chunk, columns)
    shape = jax.ShapeDtypeStruct
    dma = pltpu.SemaphoreType.DMA
    row = lambda v: v.reshape(1, -1)
    scratch = [
        pltpu.VMEM((width, columns), F32), pltpu.VMEM((columns, width), F32),
        pltpu.VMEM(cube, BF16), pltpu.VMEM(cube, BF16),
        pltpu.VMEM((2, 2, 2, chunk, columns), BF16),
        pltpu.VMEM((2, 2, chunk, columns), BF16),
        pltpu.VMEM((2, chunk, columns), BF16),
        pltpu.VMEM(cube, BF16),
        pltpu.VMEM((2, 1, width), F32), pltpu.VMEM((2, 1, chunk), F32), pltpu.VMEM((2, 1, chunk), F32),
        pltpu.VMEM((2, 2, 2, 2, vw), F32), pltpu.VMEM((2, 2, 2, vw), F32),
        pltpu.VMEM((2, 2, vw), F32), pltpu.VMEM((2, vw), F32),
    ]
    grant = sum(math.prod(s.shape) * jnp.dtype(s.dtype).itemsize for s in scratch) + GRANT_EXTRA
    hu, hd, par, sta, vg, vown = pl.pallas_call(
        functools.partial(kernel, replicas, slabs, order),
        out_shape=(
            pltpu.VMEM(cube, BF16), pltpu.VMEM((columns, width), BF16),
            pltpu.VMEM((2, chunk, columns), F32), pltpu.VMEM((2, chunk, columns), F32),
            pltpu.VMEM((2, 2, 2, 2, vw), F32), pltpu.VMEM((4, 1, chunk), F32),
        ),
        in_specs=[hbm] * 12,
        out_specs=[vmem] * 6,
        scratch_shapes=scratch + [
            dma((SH2 + 1,)), dma((4, count)), dma((3,)), dma((5,)),
            dma((count,)), dma((2,)), dma((3,)),
        ],
        compiler_params=pltpu.CompilerParams(collective_id=0, has_side_effects=True, vmem_limit_bytes=grant),
    )(*(pltpu.with_memory_space_constraint(v, pltpu.HBM) for v in (
        slope_up, slope_down, slope_norm, slope_bias,
        param_up, param_down.T, row(param_norm), row(param_bias),
        state_up, state_down.T, row(state_norm), row(state_bias),
    )))
    block, line = shape((chunk, columns), F32), shape((1, chunk), F32)
    half = shape((width,), BF16)
    hu, hd, nu, nd, tu, td, nn, nb, tn, tb, hn, hb = pl.pallas_call(
        functools.partial(spill, replicas, chunk),
        out_shape=(shape((width, columns), BF16), shape((columns, width), BF16)) + (block,) * 4 + (line,) * 4 + (half,) * 2,
        in_specs=[vmem] * 6,
        out_specs=[hbm] * 12,
        scratch_shapes=[pltpu.VMEM((width,), BF16), pltpu.VMEM((width,), BF16), dma((12,))],
        compiler_params=pltpu.CompilerParams(vmem_limit_bytes=GRANT_EXTRA),
    )(hu, hd, par, sta, vg, vown)
    flat = lambda v: v.reshape(-1)
    return hu, hd, hn, hb, nu, nd.T, flat(nn), flat(nb), tu, td.T, flat(tn), flat(tb)


def plain(slope_up, slope_down, slope_norm, slope_bias, param_up, param_down, param_norm, param_bias,
          state_up, state_down, state_norm, state_bias):
    rate = lax.axis_size("dp") ** (-0.5)
    place = lax.axis_index("dp")

    def step(mean, param, state):
        state_new = hold_rate * state + mean * rate
        return param - learn_rate * state_new, state_new

    def scattered(slope, dim):
        return lax.psum_scatter(slope[0].astype(BF16), "dp", scatter_dimension=dim, tiled=True).astype(F32)

    def gathered(value, dim):
        return lax.all_gather(value.astype(BF16), "dp", axis=dim, tiled=True)

    sums = lax.psum((slope_norm[0], slope_bias[0]), "dp")
    size = param_norm.shape[0]
    own = [lax.dynamic_slice_in_dim(v, place * size, size) for v in sums]
    nu, tu = step(scattered(slope_up, 0), param_up, state_up)
    nd, td = step(scattered(slope_down, 1), param_down, state_down)
    nn, tn = step(own[0], param_norm, state_norm)
    nb, tb = step(own[1], param_bias, state_bias)
    halves = gathered(nu, 0), gathered(nd, 1), gathered(nn, 0), gathered(nb, 0)
    return halves + (nu, nd, nn, nb, tu, td, tn, tb)


def body(*args):
    replicas = lax.axis_size("dp")
    chunk, columns = args[4].shape
    fits = replicas == 2 ** 3 and chunk % 16 == 0 and columns % (2 * LANES) == 0
    fits = fits and (replicas * chunk) % LANES == 0
    return (fused if fits else plain)(*args)


def solution(mesh):
    matrices = (P("dp", "tp"), P("tp", "dp"), P("dp"), P("dp"))
    return jax.shard_map(
        body,
        mesh=mesh,
        in_specs=(P("dp", None, "tp"), P("dp", "tp", None), P("dp", None), P("dp", None)) + matrices * 2,
        out_specs=(P(None, "tp"), P("tp", None), P(), P()) + matrices * 2,
        check_vma=False,
    )
```

time: 78.9 us -> 65.9 us (0.84)
  local copies, waits for them, and re-layouts: 12.1 us -> 0 us
    unnamed x16 -> x0, local copies, waits for them, and re-layouts: 9.28 us -> none
    slice x2 -> x0, local copies, waits for them, and re-layouts: 2.81 us -> none  [the longest x1 1.41 us: fused(): own[1, 1]]
    pallas_call x1 -> x2, Pallas kernels: 65.8 us -> 65.1 us  [the longest x1 61.2 us: fused(): pl.pallas_call(functools.partial(kernel, replicas, slabs, order), out_sha...]
where the time goes in v1:
time: 65.9 us; the launch traced here: 65.7 us
  Pallas kernels  65.1 us (99%)
  between operations  0.66 us (1%)
    pallas_call x1, Pallas kernels, fused(): pl.pallas_call(functools.partial(kernel, replicas, slabs, order), out_sha...  61.2 us
    pallas_call x1, Pallas kernels, fused(): pl.pallas_call(functools.partial(spill, replicas, chunk), out_shape=(shap...  3.91 us

profile of v1, /device:TPU:0, one launch (start us, length us, event | category | flops | bytes accessed | tf_op | source)
XLA Modules:
  0.0 65.7 jit_solution(5471591714483235556)
XLA Ops:
  0.6 61.2 %shard_map.211 = (bf16[2,2,2,160,1280]{4,3,2,1,0:T(8,128)(2,1)S(1)}, bf16[1280,1280]{1,0:T(8,128)(2,1)S(1)}, f32[2,160,1280]{2,1,0:T(8,128)S(1)}, f32[2,160,1280...) custom-call(f32[1,1280,1280]{2,1,0:T(8,128)} %su.1, f32[1,1280,1280]{2,1,0:T(8,128)} %sd.1, ...), custom_call_target="tpu_custom_call" | custom-call | tf_op jit(solution)/shard_map/pallas_call | solution.py:381
  61.8 3.9 %shard_map.212 = (bf16[1280,1280]{1,0:T(8,128)(2,1)}, bf16[1280,1280]{1,0:T(8,128)(2,1)}, f32[160,1280]{1,0:T(8,128)}, f32[160,1280]{1,0:T(8,128)}, f32[160,1280...) custom-call(bf16[2,2,2,160,1280]{4,3,2,1,0:T(8,128)(2,1)S(1)} %get-t, ...), custom_call_target="tpu_custom_call" | custom-call | tf_op jit(solution)/shard_map/pallas_call | solution.py:402

commit v2 on v1

--- a/solution.py
+++ b/solution.py
@@ -14,7 +14,7 @@
 GRANT_EXTRA = 2 * 1024 * 1024
 F32 = jnp.float32
 BF16 = jnp.bfloat16
-D2D, RS1, RS2, AG1, AG2, SH1, SH2 = range(7)
+FAR, NEAR, RS1, RS2, AG1, AG2, SH1, SH2, END, OVER = range(10)
 
 
 def widths_of(half, small):
@@ -70,11 +70,15 @@
     rate = replicas ** (-0.5)
     step = 32 if chunk % 32 == 0 else 16
     count = len(slabs)
+    per = len([s for s in slabs if s[0] == 0])
     b, g = (bu, bd), (gu, gd)
     V = count
 
+    over = tuple(peer + 1 - 2 * c for peer in nbr)
+    kept = chunk - chunk * 4 // 10 // 16 * 16
+
     barrier = pltpu.get_barrier_semaphore()
-    for peer in (mate,) + nbr:
+    for peer in (mate,) + nbr + over:
         pl.semaphore_signal(barrier, inc=1, device_id={"dp": peer}, device_id_type=pl.DeviceIdType.MESH)
 
     def local(src, dst, sem):
@@ -82,12 +86,15 @@
         cp.start()
         return cp
 
-    loads = []
-    for i, (m, lo, w, _) in enumerate(slabs):
+    loads = {}
+    for i, (m, lo, w, axis) in enumerate(slabs):
+        if i > 3 and axis == 1:
+            continue
+        span = pl.ds(lo, w if i < 4 else 2 * w)
         if m == 0:
-            loads.append(local(su.at[0, :, pl.ds(lo, w)], fu.at[:, pl.ds(lo, w)], load_sem.at[i]))
+            loads[i] = local(su.at[0, :, span], fu.at[:, span], load_sem.at[len(loads)])
         else:
-            loads.append(local(sd.at[0, pl.ds(lo, w)], fd.at[pl.ds(lo, w)], load_sem.at[i]))
+            loads[i] = local(sd.at[0, span], fd.at[span], load_sem.at[len(loads)])
     for n, (whole, pair) in enumerate(((vin, (sn, sb)), (vpar, (pn, pb)), (vsta, (tn, tb)))):
         for row in (0, 1):
             local(pair[row], whole.at[row], vec_sem.at[n])
@@ -101,7 +108,8 @@
 
     def convert(i):
         m, lo, w, _ = slabs[i]
-        loads[i].wait()
+        if i in loads:
+            loads[i].wait()
         if m == 0:
             for k in range(replicas):
                 bu[*spot(k), :, lo : lo + w] = fu[k * chunk : (k + 1) * chunk, lo : lo + w].astype(BF16)
@@ -116,15 +124,22 @@
                     bd[*spot(k), off : off + n, lo : lo + w] = turned[done : done + n]
                     done += n
 
-    share_of = {D2D: 0, AG1: 0, RS1: 1, AG2: 1, RS2: 2, SH1: 3, SH2: 3}
-    vec_out = {D2D: 0, AG2: 0, SH1: 0, RS1: 1, SH2: 1, RS2: 2, AG1: 2}
-    vec_in = {D2D: 0, AG1: 0, RS1: 1, AG2: 4, RS2: 2, SH1: 3, SH2: 3}
+    leave = {FAR: 0, NEAR: 0, AG2: 1, END: 1, SH1: 1, RS1: 2, SH2: 2, OVER: 2, RS2: 3, AG1: 3}
+    vec_out = {FAR: 0, AG2: 0, SH1: 0, RS1: 1, SH2: 1, RS2: 2, AG1: 2}
+    vec_in = {FAR: 0, AG1: 0, RS1: 1, AG2: 4, RS2: 2, SH1: 3, SH2: 3}
+
+    def arrival(i, kind):
+        if kind in (SH1, SH2, OVER):
+            return 3 * count + (1 + (i - per) // 2 if slabs[i][0] else 0)
+        if kind in (NEAR, END):
+            return 3 * count + 1 + (count - per) // 2 + (kind == END)
+        return {FAR: 0, AG1: 0, RS1: 1, AG2: 1, RS2: 2}[kind] * count + (i ^ 1 if kind == AG2 else i)
 
     def remote(i, kind, src, dst, target):
         if i == V:
             sems = vsend_sem.at[vec_out[kind]], vrecv_sem.at[vec_in[kind]]
         else:
-            sems = send_sem.at[kind], recv_sem.at[share_of[kind], i ^ 1 if kind == AG2 else i]
+            sems = send_sem.at[leave[kind]], recv_sem.at[arrival(i, kind)]
         return pltpu.make_async_remote_copy(
             src_ref=src, dst_ref=dst, send_sem=sems[0], recv_sem=sems[1],
             device_id={"dp": target}, device_id_type=pl.DeviceIdType.MESH,
@@ -139,38 +154,37 @@
     def sent(kind, whole):
         remote(0, kind, whole, whole, mate).wait_send()
 
-    def swap(i):
-        m, lo, w, _ = slabs[i]
-        cols = pl.ds(lo, w)
-        copy(i, D2D, b[m].at[:, :, 1 - c, :, cols], r0.at[m, :, :, :, cols], mate)
-
-    def add_to(dst, src, lo, w):
-        cols = slice(lo, lo + w)
-        dst[:, cols] = dst[:, cols] + src[:, cols]
-
-    def rs1(i, swap_next=None):
-        m, lo, w, axis = slabs[i]
-        cols = pl.ds(lo, w)
-        copies[i, D2D].wait_recv()
-        for far in (1, 0):
-            for j in (0, 1):
-                at = (j, 1 - fast if far else fast) if axis == 0 else (1 - slow if far else slow, j)
-                add_to(b[m].at[*at, c], r0.at[m, *at], lo, w)
-            if far:
-                src = b[m].at[:, 1 - fast, c, :, cols] if axis == 0 else b[m].at[1 - slow, :, c, :, cols]
-                copy(i, RS1, src, r1.at[m, :, :, cols], nbr[axis])
-                if swap_next is not None:
-                    swap(swap_next)
+    def swap(i, kind):
+        m, lo, w, axis = slabs[i]
+        cols = pl.ds(lo, w)
+        if axis == 0:
+            at = 1 - slow if kind == FAR else slow
+            copy(i, kind, b[m].at[:, at, 1 - c, :, cols], r0.at[m, :, at, :, cols], mate)
+        else:
+            at = 1 - fast if kind == FAR else fast
+            copy(i, kind, b[m].at[at, :, 1 - c, :, cols], r0.at[m, at, :, :, cols], mate)
+
+    def rs1(i):
+        m, lo, w, axis = slabs[i]
+        cols = pl.ds(lo, w)
+        copies[i, FAR].wait_recv()
+        for j in (0, 1):
+            at = (j, 1 - fast) if axis == 0 else (1 - slow, j)
+            b[m][*at, c, :, lo : lo + w] = b[m][*at, c, :, lo : lo + w] + r0[m, *at, :, lo : lo + w]
+        src = b[m].at[:, 1 - fast, c, :, cols] if axis == 0 else b[m].at[1 - slow, :, c, :, cols]
+        copy(i, RS1, src, r1.at[m, :, :, cols], nbr[axis])
 
     def rs2(i):
         m, lo, w, axis = slabs[i]
+        cs = slice(lo, lo + w)
         cols = pl.ds(lo, w)
         copies[i, RS1].wait_recv()
         j = 1 - slow if axis == 0 else 1 - fast
-        far = b[m].at[1 - slow, fast, c] if axis == 0 else b[m].at[slow, 1 - fast, c]
-        add_to(far, r1.at[m, j], lo, w)
-        copy(i, RS2, far.at[:, cols], r2.at[m, :, cols], nbr[1 - axis])
-        add_to(b[m].at[slow, fast, c], r1.at[m, 1 - j], lo, w)
+        far = (1 - slow, fast) if axis == 0 else (slow, 1 - fast)
+        b[m][*far, c, :, cs] = b[m][*far, c, :, cs] + r0[m, *far, :, cs] + r1[m, j, :, cs]
+        copy(i, RS2, b[m].at[*far, c, :, cols], r2.at[m, :, cols], nbr[1 - axis])
+        own = slow, fast
+        b[m][*own, c, :, cs] = b[m][*own, c, :, cs] + r0[m, *own, :, cs] + r1[m, 1 - j, :, cs]
 
     def update(i):
         m, lo, w, axis = slabs[i]
@@ -194,22 +208,33 @@
         m, lo, w, axis = slabs[i]
         cols = pl.ds(lo, w)
         copies[i, AG1].wait_recv()
-        part = g[m].at[:, fast, c, :, cols] if axis == 0 else g[m].at[slow, :, c, :, cols]
-        copy(i, AG2, part, part, nbr[axis])
-        copy(i, SH1, part, part, mate)
+        part = g[m].at[:, fast, c] if axis == 0 else g[m].at[slow, :, c]
+        early = part.at[:, pl.ds(0, kept if i < 2 else chunk), cols]
+        copy(i, AG2, early, early, nbr[axis])
+        copy(i, SH1, part.at[:, :, cols], part.at[:, :, cols], mate)
+
+    def ends():
+        for i in (0, 1):
+            m, lo, w, axis = slabs[i]
+            part = g[m].at[:, fast, c] if axis == 0 else g[m].at[slow, :, c]
+            rest = part.at[:, pl.ds(kept, chunk - kept), pl.ds(lo, w)]
+            copy(i, END, rest, rest, nbr[axis])
+            copy(i, OVER, rest, rest, over[axis])
 
     def share(i):
         m, lo, w, axis = slabs[i]
         cols = pl.ds(lo, w)
         copies[i, AG2].wait_recv()
-        part = g[m].at[:, 1 - fast, c, :, cols] if axis == 0 else g[m].at[1 - slow, :, c, :, cols]
+        part = g[m].at[:, 1 - fast, c] if axis == 0 else g[m].at[1 - slow, :, c]
+        part = part.at[:, pl.ds(0, kept if i < 2 else chunk), cols]
         copy(i, SH2, part, part, mate)
 
     def finish(i):
         m, lo, w, axis = slabs[i]
-        both = g[m].at[:, :, 1 - c, :, pl.ds(lo, w)]
-        remote(i, SH2, both, both, mate).wait_recv()
         if m == 1:
+            if axis == 0:
+                pair = gd.at[:, :, 1 - c, :, pl.ds(lo, 2 * w)]
+                remote(i, SH2, pair, pair, mate).wait_recv()
             for block in range(width // LANES):
                 first, done, parts = block * LANES, 0, []
                 while done < LANES:
@@ -225,10 +250,10 @@
         for row in (0, 1):
             for k in range(replicas):
                 vb[*spot(k), row : row + 1, 0:chunk] = vin[row, :, k * chunk : (k + 1) * chunk]
-        copy(V, D2D, vb.at[:, :, 1 - c], vr0, mate)
+        copy(V, FAR, vb.at[:, :, 1 - c], vr0, mate)
 
     def vec_rs1():
-        copies[V, D2D].wait_recv()
+        copies[V, FAR].wait_recv()
         for at in ((0, 0), (0, 1), (1, 0), (1, 1)):
             vb[*at, c] = vb[*at, c] + vr0[*at]
         copy(V, RS1, vb.at[:, 1 - fast, c], vr1, nbr[0])
@@ -264,52 +289,60 @@
     vb[...] = jnp.zeros_like(vb)
     vg[slow, fast, c] = jnp.zeros(vr2.shape, F32)
     convert(0)
-    pl.semaphore_wait(barrier, 3)
-    swap(0)
+    pl.semaphore_wait(barrier, 5)
+    swap(0, FAR)
     convert(1)
-    swap(1)
+    swap(1, FAR)
     for i in range(2, count):
         convert(i)
-        rs1(i - 2, i)
+        swap(i, FAR)
+        rs1(i - 2)
         if i == 6:
             vec_swap()
         if i == 8:
             vec_rs1()
-    rs1(count - 2)
-    rs1(count - 1)
+    for i in (count - 2, count - 1):
+        rs1(i)
+    for i in range(count):
+        swap(i, NEAR)
+    remote(0, NEAR, r1, r1, mate).wait_recv()
 
     for i in range(count):
         rs2(i)
         if i == 4:
-            sent(D2D, r0)
+            sent(FAR, r0)
+        if i == 7:
             vec_rs2()
     loaded(par_sem, par, sta)
     for n, i in enumerate(list(range(2, count)) + [0, 1]):
         update(i)
-        if n == 0:
+        if n == 6:
             vec_update()
-            sent(RS1, r1)
     for n, i in enumerate(order):
         ag2(i)
-        if n == 0:
+        if n == 4:
             vec_ag2()
-            sent(RS2, r2)
+    ends()
     for n, i in enumerate(order):
         share(i)
         if n == 0:
-            sent(AG1, r2)
-        if n == 1:
+            sent(RS2, r1)
+        if n == 5:
             vec_share()
-        if n:
-            finish(order[n - 1])
+        if n > 1:
+            finish(order[n - 2])
+    finish(order[-2])
+    finish(order[-1])
     other = vg.at[:, :, 1 - c]
     remote(V, SH2, other, other, mate).wait_recv()
-    for whole, kind in ((vb, D2D), (vr0, RS1), (vr1, RS2)):
+    for whole, kind in ((vb, FAR), (vr0, RS1), (vr1, RS2)):
         remote(V, kind, whole, whole, mate).wait_send()
-    sent(SH1, r1)
-    sent(AG2, r1)
-    finish(order[-1])
-    sent(SH2, r1)
+    rest = gu.at[:, 0, c, pl.ds(kept, chunk - kept), pl.ds(0, 2 * slabs[0][2])]
+    remote(0, END, rest, rest, mate).wait_recv()
+    whole = gu.at[:, :, 1 - c]
+    remote(0, SH2, whole, whole, mate).wait_recv()
+    sent(AG2, r0)
+    sent(SH2, r0)
 
 
 def spill(
@@ -388,8 +421,8 @@
         in_specs=[hbm] * 12,
         out_specs=[vmem] * 6,
         scratch_shapes=scratch + [
-            dma((SH2 + 1,)), dma((4, count)), dma((3,)), dma((5,)),
-            dma((count,)), dma((2,)), dma((3,)),
+            dma((4,)), dma((3 * count + 3 + (count - per) // 2,)), dma((3,)), dma((5,)),
+            dma((2 + count // 2,)), dma((2,)), dma((3,)),
         ],
         compiler_params=pltpu.CompilerParams(collective_id=0, has_side_effects=True, vmem_limit_bytes=grant),
     )(*(pltpu.with_memory_space_constraint(v, pltpu.HBM) for v in (

time: 65.9 us -> 65.4 us (level)
  no operation moved by 1% of the time
where the time goes in v2:
time: 65.4 us; the launch traced here: 65.2 us
  Pallas kernels  64.5 us (99%)
  between operations  0.66 us (1%)
    pallas_call x1, Pallas kernels, fused(): pl.pallas_call(functools.partial(kernel, replicas, slabs, order), out_sha...  60.6 us
    pallas_call x1, Pallas kernels, fused(): pl.pallas_call(functools.partial(spill, replicas, chunk), out_shape=(shap...  3.91 us

profile of v2, /device:TPU:0, one launch (start us, length us, event | category | flops | bytes accessed | tf_op | source)
XLA Modules:
  0.0 65.2 jit_solution(7011418168534241531)
XLA Ops:
  0.6 60.6 %shard_map.211 = (bf16[2,2,2,160,1280]{4,3,2,1,0:T(8,128)(2,1)S(1)}, bf16[1280,1280]{1,0:T(8,128)(2,1)S(1)}, f32[2,160,1280]{2,1,0:T(8,128)S(1)}, f32[2,160,1280...) custom-call(f32[1,1280,1280]{2,1,0:T(8,128)} %su.1, f32[1,1280,1280]{2,1,0:T(8,128)} %sd.1, ...), custom_call_target="tpu_custom_call" | custom-call | tf_op jit(solution)/shard_map/pallas_call | solution.py:414
  61.3 3.9 %shard_map.212 = (bf16[1280,1280]{1,0:T(8,128)(2,1)}, bf16[1280,1280]{1,0:T(8,128)(2,1)}, f32[160,1280]{1,0:T(8,128)}, f32[160,1280]{1,0:T(8,128)}, f32[160,1280...) custom-call(bf16[2,2,2,160,1280]{4,3,2,1,0:T(8,128)(2,1)S(1)} %get-t, ...), custom_call_target="tpu_custom_call" | custom-call | tf_op jit(solution)/shard_map/pallas_call | solution.py:435

commit v3 on v2

--- a/solution.py
+++ b/solution.py
@@ -78,7 +78,7 @@
     kept = chunk - chunk * 4 // 10 // 16 * 16
 
     barrier = pltpu.get_barrier_semaphore()
-    for peer in (mate,) + nbr + over:
+    for peer in (mate,) + nbr:
         pl.semaphore_signal(barrier, inc=1, device_id={"dp": peer}, device_id_type=pl.DeviceIdType.MESH)
 
     def local(src, dst, sem):
@@ -289,14 +289,17 @@
     vb[...] = jnp.zeros_like(vb)
     vg[slow, fast, c] = jnp.zeros(vr2.shape, F32)
     convert(0)
-    pl.semaphore_wait(barrier, 5)
+    pl.semaphore_wait(barrier, 3)
     swap(0, FAR)
     convert(1)
     swap(1, FAR)
+    rs1(0)
+    rs1(1)
     for i in range(2, count):
         convert(i)
         swap(i, FAR)
-        rs1(i - 2)
+        if i > 3:
+            rs1(i - 2)
         if i == 6:
             vec_swap()
         if i == 8:

time: 65.4 us -> 65.1 us (level)
  no operation moved by 1% of the time
where the time goes in v3:
time: 65.1 us; the launch traced here: 65 us
  Pallas kernels  64.3 us (99%)
  between operations  0.66 us (1%)
    pallas_call x1, Pallas kernels, fused(): pl.pallas_call(functools.partial(kernel, replicas, slabs, order), out_sha...  60.4 us
    pallas_call x1, Pallas kernels, fused(): pl.pallas_call(functools.partial(spill, replicas, chunk), out_shape=(shap...  3.91 us

profile of v3, /device:TPU:0, one launch (start us, length us, event | category | flops | bytes accessed | tf_op | source)
XLA Modules:
  0.0 65.0 jit_solution(3273989256193428639)
XLA Ops:
  0.6 60.4 %shard_map.211 = (bf16[2,2,2,160,1280]{4,3,2,1,0:T(8,128)(2,1)S(1)}, bf16[1280,1280]{1,0:T(8,128)(2,1)S(1)}, f32[2,160,1280]{2,1,0:T(8,128)S(1)}, f32[2,160,1280...) custom-call(f32[1,1280,1280]{2,1,0:T(8,128)} %su.1, f32[1,1280,1280]{2,1,0:T(8,128)} %sd.1, ...), custom_call_target="tpu_custom_call" | custom-call | tf_op jit(solution)/shard_map/pallas_call | solution.py:417
  61.1 3.9 %shard_map.212 = (bf16[1280,1280]{1,0:T(8,128)(2,1)}, bf16[1280,1280]{1,0:T(8,128)(2,1)}, f32[160,1280]{1,0:T(8,128)}, f32[160,1280]{1,0:T(8,128)}, f32[160,1280...) custom-call(bf16[2,2,2,160,1280]{4,3,2,1,0:T(8,128)(2,1)S(1)} %get-t, ...), custom_call_target="tpu_custom_call" | custom-call | tf_op jit(solution)/shard_map/pallas_call | solution.py:438

commit v4 on v3

--- a/solution.py
+++ b/solution.py
@@ -128,12 +128,14 @@
     vec_out = {FAR: 0, AG2: 0, SH1: 0, RS1: 1, SH2: 1, RS2: 2, AG1: 2}
     vec_in = {FAR: 0, AG1: 0, RS1: 1, AG2: 4, RS2: 2, SH1: 3, SH2: 3}
 
+    half = count // 2
+
     def arrival(i, kind):
         if kind in (SH1, SH2, OVER):
-            return 3 * count + (1 + (i - per) // 2 if slabs[i][0] else 0)
+            return 2 * count + (1 + (i - per) // 2 if slabs[i][0] else 0)
         if kind in (NEAR, END):
-            return 3 * count + 1 + (count - per) // 2 + (kind == END)
-        return {FAR: 0, AG1: 0, RS1: 1, AG2: 1, RS2: 2}[kind] * count + (i ^ 1 if kind == AG2 else i)
+            return 2 * count + 1 + (count - per) // 2 + (kind == END)
+        return i if kind in (FAR, AG1) else count + i // 2 + (half if kind == RS2 else 0)
 
     def remote(i, kind, src, dst, target):
         if i == V:
@@ -147,6 +149,17 @@
 
     copies = {}
 
+    def arrived(i, kind):
+        m, lo, w, axis = slabs[i]
+        if axis:
+            return
+        cols = pl.ds(lo, 2 * w)
+        if kind == RS2:
+            whole = r2.at[m, :, cols]
+        else:
+            whole = r1.at[m, :, pl.ds(0, kept if kind == AG2 and i < 2 else chunk), cols]
+        remote(i, kind, whole, whole, mate).wait_recv()
+
     def copy(i, kind, src, dst, target):
         copies[i, kind] = remote(i, kind, src, dst, target)
         copies[i, kind].start()
@@ -178,7 +191,7 @@
         m, lo, w, axis = slabs[i]
         cs = slice(lo, lo + w)
         cols = pl.ds(lo, w)
-        copies[i, RS1].wait_recv()
+        arrived(i, RS1)
         j = 1 - slow if axis == 0 else 1 - fast
         far = (1 - slow, fast) if axis == 0 else (slow, 1 - fast)
         b[m][*far, c, :, cs] = b[m][*far, c, :, cs] + r0[m, *far, :, cs] + r1[m, j, :, cs]
@@ -190,7 +203,7 @@
         m, lo, w, axis = slabs[i]
         cs = slice(lo, lo + w)
         cols = pl.ds(lo, w)
-        copies[i, RS2].wait_recv()
+        arrived(i, RS2)
         own, out = b[m].at[slow, fast, c], g[m].at[slow, fast, c]
 
         def go(rows):
@@ -224,7 +237,7 @@
     def share(i):
         m, lo, w, axis = slabs[i]
         cols = pl.ds(lo, w)
-        copies[i, AG2].wait_recv()
+        arrived(i, AG2)
         part = g[m].at[:, 1 - fast, c] if axis == 0 else g[m].at[1 - slow, :, c]
         part = part.at[:, pl.ds(0, kept if i < 2 else chunk), cols]
         copy(i, SH2, part, part, mate)
@@ -296,9 +309,11 @@
     rs1(0)
     rs1(1)
     for i in range(2, count):
+        if i == 4:
+            rs1(2)
         convert(i)
         swap(i, FAR)
-        if i > 3:
+        if i > 4:
             rs1(i - 2)
         if i == 6:
             vec_swap()
@@ -332,14 +347,15 @@
             sent(RS2, r1)
         if n == 5:
             vec_share()
+        if n == count - 2:
+            other = vg.at[:, :, 1 - c]
+            remote(V, SH2, other, other, mate).wait_recv()
+            for whole, kind in ((vb, FAR), (vr0, RS1), (vr1, RS2)):
+                remote(V, kind, whole, whole, mate).wait_send()
         if n > 1:
             finish(order[n - 2])
     finish(order[-2])
     finish(order[-1])
-    other = vg.at[:, :, 1 - c]
-    remote(V, SH2, other, other, mate).wait_recv()
-    for whole, kind in ((vb, FAR), (vr0, RS1), (vr1, RS2)):
-        remote(V, kind, whole, whole, mate).wait_send()
     rest = gu.at[:, 0, c, pl.ds(kept, chunk - kept), pl.ds(0, 2 * slabs[0][2])]
     remote(0, END, rest, rest, mate).wait_recv()
     whole = gu.at[:, :, 1 - c]
@@ -424,7 +440,7 @@
         in_specs=[hbm] * 12,
         out_specs=[vmem] * 6,
         scratch_shapes=scratch + [
-            dma((4,)), dma((3 * count + 3 + (count - per) // 2,)), dma((3,)), dma((5,)),
+            dma((4,)), dma((2 * count + 3 + (count - per) // 2,)), dma((3,)), dma((5,)),
             dma((2 + count // 2,)), dma((2,)), dma((3,)),
         ],
         compiler_params=pltpu.CompilerParams(collective_id=0, has_side_effects=True, vmem_limit_bytes=grant),

time: 65.1 us -> 65.1 us (level)
  no operation moved by 1% of the time
where the time goes in v4:
time: 65.1 us; the launch traced here: 65 us
  Pallas kernels  64.3 us (99%)
  between operations  0.66 us (1%)
    pallas_call x1, Pallas kernels, fused(): pl.pallas_call(functools.partial(kernel, replicas, slabs, order), out_sha...  60.4 us
    pallas_call x1, Pallas kernels, fused(): pl.pallas_call(functools.partial(spill, replicas, chunk), out_shape=(shap...  3.91 us

profile of v4, /device:TPU:0, one launch (start us, length us, event | category | flops | bytes accessed | tf_op | source)
XLA Modules:
  0.0 65.0 jit_solution(8979545586811302964)
XLA Ops:
  0.6 60.4 %shard_map.211 = (bf16[2,2,2,160,1280]{4,3,2,1,0:T(8,128)(2,1)S(1)}, bf16[1280,1280]{1,0:T(8,128)(2,1)S(1)}, f32[2,160,1280]{2,1,0:T(8,128)S(1)}, f32[2,160,1280...) custom-call(f32[1,1280,1280]{2,1,0:T(8,128)} %su.1, f32[1,1280,1280]{2,1,0:T(8,128)} %sd.1, ...), custom_call_target="tpu_custom_call" | custom-call | tf_op jit(solution)/shard_map/pallas_call | solution.py:433
  61.0 3.9 %shard_map.212 = (bf16[1280,1280]{1,0:T(8,128)(2,1)}, bf16[1280,1280]{1,0:T(8,128)(2,1)}, f32[160,1280]{1,0:T(8,128)}, f32[160,1280]{1,0:T(8,128)}, f32[160,1280...) custom-call(bf16[2,2,2,160,1280]{4,3,2,1,0:T(8,128)(2,1)S(1)} %get-t, ...), custom_call_target="tpu_custom_call" | custom-call | tf_op jit(solution)/shard_map/pallas_call | solution.py:454

commit v5 on v4

--- a/solution.py
+++ b/solution.py
@@ -191,7 +191,8 @@
         m, lo, w, axis = slabs[i]
         cs = slice(lo, lo + w)
         cols = pl.ds(lo, w)
-        arrived(i, RS1)
+        if i >= 4:
+            arrived(i, RS1)
         j = 1 - slow if axis == 0 else 1 - fast
         far = (1 - slow, fast) if axis == 0 else (slow, 1 - fast)
         b[m][*far, c, :, cs] = b[m][*far, c, :, cs] + r0[m, *far, :, cs] + r1[m, j, :, cs]
@@ -321,6 +322,8 @@
             vec_rs1()
     for i in (count - 2, count - 1):
         rs1(i)
+    for i in range(4):
+        arrived(i, RS1)
     for i in range(count):
         swap(i, NEAR)
     remote(0, NEAR, r1, r1, mate).wait_recv()

time: 65.1 us -> 65.1 us (level)
  no operation moved by 1% of the time
where the time goes in v5:
time: 65.1 us; the launch traced here: 65 us
  Pallas kernels  64.3 us (99%)
  between operations  0.66 us (1%)
    pallas_call x1, Pallas kernels, fused(): pl.pallas_call(functools.partial(kernel, replicas, slabs, order), out_sha...  60.4 us
    pallas_call x1, Pallas kernels, fused(): pl.pallas_call(functools.partial(spill, replicas, chunk), out_shape=(shap...  3.91 us

profile of v5, /device:TPU:0, one launch (start us, length us, event | category | flops | bytes accessed | tf_op | source)
XLA Modules:
  0.0 65.0 jit_solution(7787116314069357055)
XLA Ops:
  0.6 60.4 %shard_map.211 = (bf16[2,2,2,160,1280]{4,3,2,1,0:T(8,128)(2,1)S(1)}, bf16[1280,1280]{1,0:T(8,128)(2,1)S(1)}, f32[2,160,1280]{2,1,0:T(8,128)S(1)}, f32[2,160,1280...) custom-call(f32[1,1280,1280]{2,1,0:T(8,128)} %su.1, f32[1,1280,1280]{2,1,0:T(8,128)} %sd.1, ...), custom_call_target="tpu_custom_call" | custom-call | tf_op jit(solution)/shard_map/pallas_call | solution.py:436
  61.0 3.9 %shard_map.212 = (bf16[1280,1280]{1,0:T(8,128)(2,1)}, bf16[1280,1280]{1,0:T(8,128)(2,1)}, f32[160,1280]{1,0:T(8,128)}, f32[160,1280]{1,0:T(8,128)}, f32[160,1280...) custom-call(bf16[2,2,2,160,1280]{4,3,2,1,0:T(8,128)(2,1)S(1)} %get-t, ...), custom_call_target="tpu_custom_call" | custom-call | tf_op jit(solution)/shard_map/pallas_call | solution.py:457
